TPU v7x, 32 devices: a whole 2x2x4 slice. The times are simulated.
32 devices in a mesh: outer: 8 (over z, x), inner: 4 (over y, core).
Axes of the slice: x: 2, y: 2, z: 4, core: 2. Of those that a mesh axis runs over, the one named last changes fastest.
Arguments:
- queries: bfloat16 [1024, 2, 4096], P('outer', None, 'inner'), may hold values from -52 to 52
- keys: bfloat16 [1024, 2, 4096], P('outer', None, 'inner'), may hold values from -6 to 6
- values: bfloat16 [1024, 2, 4096], P('outer', None, 'inner'), may hold values from -6 to 6
Outputs:
- attended: bfloat16 [1024, 2, 4096], P(('outer', 'inner'))
All inputs are finite; a program needn't handle non-finite values.
Results may differ from a plain program's by a relative error of at most 0.004.
Values may be sent and summed in bfloat16 or wider, within the bound.
A program may use at most 128 MiB of HBM per device.

v0:
```python
from functools import partial
import math

import jax
import jax.numpy as jnp
from jax import lax
from jax.sharding import PartitionSpec as P

HEAD_DIM = 128


def attend_keys(running, key_block, value_block, query_heads, head_count):
    peak_rows, totals, numerator = running
    key_count = key_block.shape[0]
    key_heads = key_block.reshape(key_count, head_count, HEAD_DIM)
    value_heads = value_block.reshape(key_count, head_count, HEAD_DIM)
    scores = jnp.einsum(
        "qhd,khd->qhk", query_heads, key_heads, preferred_element_type=jnp.float32
    ) * (1.0 / math.sqrt(HEAD_DIM))
    new_peaks = jnp.maximum(peak_rows, jnp.max(scores, axis=2))
    shrink = jnp.exp(peak_rows - new_peaks)
    weights = jnp.exp(scores - new_peaks[..., None])
    totals = totals * shrink + jnp.sum(weights, axis=2)
    numerator = numerator * shrink[..., None] + jnp.einsum(
        "qhk,khd->qhd",
        weights.astype(jnp.bfloat16),
        value_heads,
        preferred_element_type=jnp.float32,
    )
    return (new_peaks, totals, numerator)


def attend_piece(running, pieces, start_row, query_part, head_count):
    key_rows, value_rows = pieces
    row_count = query_part.shape[0]
    query_heads = query_part.reshape(row_count, head_count, HEAD_DIM)
    block_count = key_rows.shape[0] // row_count
    key_blocks = key_rows.reshape(block_count, row_count, key_rows.shape[1])
    value_blocks = value_rows.reshape(block_count, row_count, value_rows.shape[1])

    def one_block(state, blocks):
        return (attend_keys(state, blocks[0], blocks[1], query_heads, head_count), None)

    running, unused = lax.scan(one_block, running, (key_blocks, value_blocks))
    return running


def start_state(row_count, head_count):
    peak_rows = jnp.full((row_count, head_count), -1e30, jnp.float32)
    totals = jnp.zeros((row_count, head_count), jnp.float32)
    numerator = jnp.zeros((row_count, head_count, HEAD_DIM), jnp.float32)
    return (peak_rows, totals, numerator)


def finish_state(running):
    peak_rows, totals, numerator = running
    averaged = numerator / totals[..., None]
    return averaged.reshape(numerator.shape[0], -1).astype(jnp.bfloat16)


def flatten(array):
    return array.reshape(array.shape[0], array.shape[1] * array.shape[2])


def per_device(queries, keys, values):
    tok_rows, networks, local_cols = queries.shape
    full_q, full_k, full_v = (
        lax.all_to_all(queries, "inner", split_axis=0, concat_axis=2, tiled=True),
        lax.all_to_all(keys, "inner", split_axis=0, concat_axis=2, tiled=True),
        lax.all_to_all(values, "inner", split_axis=0, concat_axis=2, tiled=True),
    )
    unit_rows = full_q.shape[0]
    full_cols = full_q.shape[2]
    query_part, key_part, value_part = (
        lax.all_to_all(flatten(full_q), "outer", split_axis=1, concat_axis=0, tiled=True),
        lax.all_to_all(flatten(full_k), "outer", split_axis=1, concat_axis=0, tiled=True),
        lax.all_to_all(flatten(full_v), "outer", split_axis=1, concat_axis=0, tiled=True),
    )
    head_count = query_part.shape[1] // HEAD_DIM
    folder = partial(attend_piece, query_part=query_part, head_count=head_count)
    running = folder(
        start_state(query_part.shape[0], head_count),
        (
            lax.all_gather(key_part, "inner", axis=0, tiled=True),
            lax.all_gather(value_part, "inner", axis=0, tiled=True),
        ),
        jnp.int32(0),
    )
    gathered = lax.all_to_all(
        finish_state(running), "outer", split_axis=0, concat_axis=1, tiled=True
    )
    attended = gathered.reshape(unit_rows, networks, full_cols)
    return attended


def solution(mesh):
    return jax.shard_map(
        per_device,
        mesh=mesh,
        in_specs=(P("outer", None, "inner"), P("outer", None, "inner"), P("outer", None, "inner")),
        out_specs=P(("outer", "inner"), None, None),
        check_vma=False,
    )
```

profile of v0, /device:TPU:0, one launch (start us, length us, event | category | flops | bytes accessed | tf_op | source)
XLA Modules:
  0.0 146.4 jit_solution(7811544565537679665)
XLA Ops:
  6.5 13.2 %all_to_all.112 = bf16[128,2,1024]{2,1,0:T(2,128)(2,1)S(1)} all-to-all(bf16[128,2,1024]{2,1,0:T(2,128)(2,1)} %param.6), channel_id=1, replica_groups=mesh['outer'=8,'inner'=4] {'inner'}, dimensions={0} | all-to-all | bytes 1048576 | tf_op jit(solution)/shard_map/all_to_all | solution.py:69
  19.9 20.5 %all_to_all.113 = bf16[32,8,1024]{2,0,1:T(8,128)(2,1)} all-to-all(bf16[32,8,1024]{2,0,1:T(8,128)(2,1)S(1)} %bitcast.72), channel_id=1, replica_groups=mesh['outer'=8,'inner'=4] {'outer'}, dimensions={1} | all-to-all | bytes 1048576 | tf_op jit(solution)/shard_map/all_to_all | solution.py:76
  40.4 14.9 %all_to_all.114 = bf16[128,2,1024]{2,1,0:T(2,128)(2,1)S(1)} all-to-all(bf16[128,2,1024]{2,1,0:T(2,128)(2,1)S(1)} %copy-done), channel_id=1, replica_groups=mesh['outer'=8,'inner'=4] {'inner'}, dimensions={0} | all-to-all | bytes 1048576 | tf_op jit(solution)/shard_map/all_to_all | solution.py:70
  55.5 17.2 %all_to_all.115 = bf16[32,8,1024]{2,0,1:T(8,128)(2,1)} all-to-all(bf16[32,8,1024]{2,0,1:T(8,128)(2,1)S(1)} %bitcast.73), channel_id=1, replica_groups=mesh['outer'=8,'inner'=4] {'outer'}, dimensions={1} | all-to-all | bytes 1048576 | tf_op jit(solution)/shard_map/all_to_all | solution.py:77
  72.7 14.9 %all_to_all.116 = bf16[128,2,1024]{2,1,0:T(2,128)(2,1)S(1)} all-to-all(bf16[128,2,1024]{2,1,0:T(2,128)(2,1)S(1)} %copy-done.1), channel_id=1, replica_groups=mesh['outer'=8,'inner'=4] {'inner'}, dimensions={0} | all-to-all | bytes 1048576 | tf_op jit(solution)/shard_map/all_to_all | solution.py:68
  87.5 0.9 copy.17
  88.5 3.5 %all-to-all-start.3 = ((bf16[32,8,1024]{2,0,1:T(8,128)(2,1)}), bf16[32,8,1024]{2,0,1:T(8,128)(2,1)S(1)}, u32[]{:S(2)}, u32[]{:S(2)}) async-start(bf16[32,8,1024]{2,0,1:T(8,128)(2,1)} %bitcast.8), calls=%async_computation.3 | async-start | bytes 1048576 | tf_op jit(solution)/shard_map/all_to_all | solution.py:75
  92.0 14.0 %all-to-all-done.3 = bf16[32,8,1024]{2,0,1:T(8,128)(2,1)S(1)} async-done(((bf16[32,8,1024]{2,0,1:T(8,128)(2,1)}), bf16[32,8,1024]{2,0,1:T(8,128)(2,1)S(1)}, u32[]{:S(2)}, u32[]{:S(2)}) %all-to-all-start.3) | async-done | bytes 524320 | tf_op jit(solution)/shard_map/all_to_all | solution.py:75
  106.3 13.4 %while.15 = (s32[]{:T(128)}, f32[256,8]{0,1:T(8,128)S(1)}, f32[256,8]{0,1:T(8,128)S(1)}, f32[256,8,128]{0,2,1:T(8,128)S(1)}, bf16[4,256,1024]{2,1,0:T(8,128)(2,1...) while((s32[]{:T(128)}, f32[256,8]{0,1:T(8,128)S(1)}, ...), condition=%wide.region_3.4_spmd.clone, body=%wide.region_0.3_spmd.clone.sunk | while | flops 273426432 | bytes 14286965 | solution.py:44
  106.3 1.3 constant_dynamic-slice_fusion.3
  108.0 0.5 bitcast_reduce_fusion.2
  108.5 0.4 fusion.23
  108.9 0.7 fusion.25
  109.6 1.3 constant_dynamic-slice_fusion.3
  111.3 0.5 bitcast_reduce_fusion.2
  112.2 0.7 fusion.25
  113.0 1.3 constant_dynamic-slice_fusion.3
  114.7 0.5 bitcast_reduce_fusion.2
  115.6 0.7 fusion.25
  116.3 1.3 constant_dynamic-slice_fusion.3
  118.0 0.5 bitcast_reduce_fusion.2
  118.9 0.7 fusion.25
  120.3 17.9 %all_to_all.117 = bf16[8,32,1024]{2,1,0:T(8,128)(2,1)S(1)} all-to-all(bf16[8,32,1024]{2,1,0:T(8,128)(2,1)S(1)} %convert_element_type.11), channel_id=1, replica_groups=mesh['outer'=8,'inner'=4] {'outer'}, dimensions={0} | all-to-all | bytes 1048576 | tf_op jit(solution)/shard_map/all_to_all | solution.py:89
  138.5 1.1 reshape.52
  (44 shorter events, 4.2 us)
Async XLA Ops:
  6.5 33.9 %copy-start = (bf16[128,2,1024]{2,1,0:T(2,128)(2,1)S(1)}, bf16[128,2,1024]{2,1,0:T(2,128)(2,1)}, u32[]{:S(2)}) copy-start(bf16[128,2,1024]{2,1,0:T(2,128)(2,1)} %param.7) | copy-start | bytes 1572868
  6.5 99.7 %all-gather.3.cloned.1.call-start = ((), (), s32[]{:S(2)}) async-start(), calls=%async_computation.7 | async-start | bytes 2621440 | tf_op jit(solution)/shard_map/all_gather | solution.py:84
  40.3 32.3 %copy-start.1 = (bf16[128,2,1024]{2,1,0:T(2,128)(2,1)S(1)}, bf16[128,2,1024]{2,1,0:T(2,128)(2,1)}, u32[]{:S(2)}) copy-start(bf16[128,2,1024]{2,1,0:T(2,128)(2,1)} %param.5) | copy-start | bytes 1572868
  40.4 65.9 %all-gather.5.cloned.1.call-start = ((), (), s32[]{:S(2)}) async-start(), calls=%async_computation.8 | async-start | bytes 2621440 | tf_op jit(solution)/shard_map/all_gather | solution.py:85
  88.5 17.6 %all-to-all-start.3 = ((bf16[32,8,1024]{2,0,1:T(8,128)(2,1)}), bf16[32,8,1024]{2,0,1:T(8,128)(2,1)S(1)}, u32[]{:S(2)}, u32[]{:S(2)}) async-start(bf16[32,8,1024]{2,0,1:T(8,128)(2,1)} %bitcast.8), calls=%async_computation.3 | async-start | bytes 1048576 | tf_op jit(solution)/shard_map/all_to_all | solution.py:75
Sparse Core Ops, SparseCore 0:
  40.5 24.0 all-gather.2
  72.8 23.8 all-gather.4
where the time goes:
time: 147 us; the launch traced here: 146 us
  blocking collectives  98.5 us (67%)
  waiting for transfers between devices  14.1 us (10%)
  between operations  13.5 us (9%)
  local copies, waits for them, and re-layouts  10 us (7%)
  matrix products  4.86 us (3%)
  starting transfers between devices  3.54 us (2%)
  other arithmetic  1.62 us (1%)
    all_to_all x1, blocking collectives, per_device(): lax.all_to_all(flatten(full_k), 'outer', split_axis=1, concat_axis=0, til...  20.5 us
    all_to_all x1, blocking collectives, per_device(): lax.all_to_all(finish_state(running), 'outer', split_axis=0, concat_axis=...  17.9 us
    all_to_all x1, blocking collectives, per_device(): lax.all_to_all(flatten(full_v), 'outer', split_axis=1, concat_axis=0, til...  17.2 us
    all_to_all x1, blocking collectives, per_device(): lax.all_to_all(values, 'inner', split_axis=0, concat_axis=2, tiled=True)  14.9 us
    all_to_all x1, blocking collectives, per_device(): lax.all_to_all(queries, 'inner', split_axis=0, concat_axis=2, tiled=True)  14.9 us
    all_to_all x1, waiting for transfers between devices, per_device(): lax.all_to_all(flatten(full_q), 'outer', split_axis=1, concat_axis=0, til...  14 us
    all_to_all x1, blocking collectives, per_device(): lax.all_to_all(keys, 'inner', split_axis=0, concat_axis=2, tiled=True)  13.2 us
    dynamic_slice x12, local copies, waits for them, and re-layouts, attend_piece(): running, unused = lax.scan(one_block, running, (key_blocks, value_blocks))  6.72 us
  transfers between devices with their start and end apart: 3, of which 1 were waited for; matrix products, arithmetic and copies ran while one was open for 1% of the time, Pallas kernels for 0%

commit v1 on v0

--- a/solution.py
+++ b/solution.py
@@ -4,9 +4,12 @@
 import jax
 import jax.numpy as jnp
 from jax import lax
+from jax.experimental import pallas as pl
+from jax.experimental.pallas import tpu as pltpu
 from jax.sharding import PartitionSpec as P
 
 HEAD_DIM = 128
+MESH = pl.DeviceIdType.MESH
 
 
 def attend_keys(running, key_block, value_block, query_heads, head_count):
@@ -30,7 +33,7 @@
     return (new_peaks, totals, numerator)
 
 
-def attend_piece(running, pieces, start_row, query_part, head_count):
+def attend_piece(running, pieces, query_part, head_count):
     key_rows, value_rows = pieces
     row_count = query_part.shape[0]
     query_heads = query_part.reshape(row_count, head_count, HEAD_DIM)
@@ -46,7 +49,7 @@
 
 
 def start_state(row_count, head_count):
-    peak_rows = jnp.full((row_count, head_count), -1e30, jnp.float32)
+    peak_rows = jnp.full((row_count, head_count), -jnp.inf, jnp.float32)
     totals = jnp.zeros((row_count, head_count), jnp.float32)
     numerator = jnp.zeros((row_count, head_count, HEAD_DIM), jnp.float32)
     return (peak_rows, totals, numerator)
@@ -62,42 +65,233 @@
     return array.reshape(array.shape[0], array.shape[1] * array.shape[2])
 
 
-def per_device(queries, keys, values):
+def per_device_split(queries, keys, values):
     tok_rows, networks, local_cols = queries.shape
     full_q, full_k, full_v = (
-        lax.all_to_all(queries, "inner", split_axis=0, concat_axis=2, tiled=True),
-        lax.all_to_all(keys, "inner", split_axis=0, concat_axis=2, tiled=True),
-        lax.all_to_all(values, "inner", split_axis=0, concat_axis=2, tiled=True),
+        lax.all_to_all(array, "inner", split_axis=0, concat_axis=2, tiled=True)
+        for array in (queries, keys, values)
     )
     unit_rows = full_q.shape[0]
     full_cols = full_q.shape[2]
     query_part, key_part, value_part = (
-        lax.all_to_all(flatten(full_q), "outer", split_axis=1, concat_axis=0, tiled=True),
-        lax.all_to_all(flatten(full_k), "outer", split_axis=1, concat_axis=0, tiled=True),
-        lax.all_to_all(flatten(full_v), "outer", split_axis=1, concat_axis=0, tiled=True),
+        lax.all_to_all(flatten(array), "outer", split_axis=1, concat_axis=0, tiled=True)
+        for array in (full_q, full_k, full_v)
     )
     head_count = query_part.shape[1] // HEAD_DIM
-    folder = partial(attend_piece, query_part=query_part, head_count=head_count)
-    running = folder(
+    running = attend_piece(
         start_state(query_part.shape[0], head_count),
         (
             lax.all_gather(key_part, "inner", axis=0, tiled=True),
             lax.all_gather(value_part, "inner", axis=0, tiled=True),
         ),
-        jnp.int32(0),
+        query_part,
+        head_count,
     )
     gathered = lax.all_to_all(
         finish_state(running), "outer", split_axis=0, concat_axis=1, tiled=True
     )
-    attended = gathered.reshape(unit_rows, networks, full_cols)
-    return attended
+    return gathered.reshape(unit_rows, networks, full_cols)
+
+
+def attend_block(query, key, value):
+    raw = lax.dot_general(
+        query, key, (((1,), (1,)), ((), ())), preferred_element_type=jnp.float32
+    )
+    peak = jnp.max(raw, axis=1, keepdims=True)
+    weights = jnp.exp2((raw - peak) * (math.log2(math.e) / math.sqrt(HEAD_DIM)))
+    totals = jnp.sum(weights, axis=1, keepdims=True)
+    numerator = jnp.dot(
+        weights.astype(jnp.bfloat16), value, preferred_element_type=jnp.float32
+    )
+    return (numerator / totals).astype(jnp.bfloat16)
+
+
+def exchange_kernel(
+    outer, inner, networks, local_heads, per,
+    q_ref, k_ref, v_ref, out_ref,
+    q_buf, k_buf, v_buf, o_buf,
+    local_sem, in_send, in_recv, out_send, out_recv,
+):
+    me_o, me_i = lax.axis_index("outer"), lax.axis_index("inner")
+    tokens = q_ref.shape[1]
+    out_rows = out_ref.shape[1]
+    all_heads = local_heads * inner
+    half = outer // 2
+    my_half, my_rest = me_o // half, me_o % half
+    refs, bufs = (k_ref, v_ref, q_ref), (k_buf, v_buf, q_buf)
+
+    def partner(step, sign):
+        side = jnp.where(step < half, 1 - my_half, my_half)
+        return side * half + (my_rest + sign * step + 2 * outer) % half
+
+    def rows_of(block):
+        return pl.ds(pl.multiple_of(block * tokens, tokens), tokens)
+
+    steps = [step for step in range(outer) if step != half]
+
+    def in_copy(unit, which, step, sign):
+        other = partner(step, sign)
+        target = other if sign == 1 else me_o
+        source = me_o if sign == 1 else other
+        return pltpu.make_async_remote_copy(
+            src_ref=refs[which].at[target * per + unit],
+            dst_ref=bufs[which].at[unit, rows_of(source)],
+            send_sem=in_send.at[unit * 3 + which, step],
+            recv_sem=in_recv.at[unit * 3 + which, step],
+            device_id=(other, me_i),
+            device_id_type=MESH,
+        )
+
+    def own_copy(unit, which):
+        return pltpu.make_async_copy(
+            refs[which].at[me_o * per + unit],
+            bufs[which].at[unit, rows_of(me_o)],
+            local_sem.at[unit * 3 + which],
+        )
+
+    def slot_of(source_o, source_i, unit):
+        pair = source_o * per + unit
+        return (pair // local_heads) * all_heads + source_i * local_heads + pair % local_heads
+
+    def out_copy(unit, block, part):
+        return pltpu.make_async_remote_copy(
+            src_ref=o_buf.at[unit, pl.ds(pl.multiple_of(block * tokens + part * out_rows, out_rows), out_rows)],
+            dst_ref=out_ref.at[slot_of(me_o, me_i, unit)],
+            send_sem=out_send.at[unit, block * inner + part],
+            recv_sem=out_recv.at[slot_of(me_o, me_i, unit)],
+            device_id=(block, part),
+            device_id_type=MESH,
+        )
+
+    def out_own(unit):
+        return pltpu.make_async_copy(
+            o_buf.at[unit, pl.ds(pl.multiple_of(me_o * tokens + me_i * out_rows, out_rows), out_rows)],
+            out_ref.at[slot_of(me_o, me_i, unit)],
+            out_recv.at[slot_of(me_o, me_i, unit)],
+        )
+
+    barrier = pltpu.get_barrier_semaphore()
+
+    def greet(index, carry):
+        other = (me_o * inner + me_i + index) % (outer * inner)
+        pl.semaphore_signal(
+            barrier, inc=1, device_id=(other // inner, other % inner), device_id_type=MESH
+        )
+        return carry
+
+    lax.fori_loop(1, outer * inner, greet, 0)
+    for unit in range(per):
+        for which in range(3):
+            own_copy(unit, which).start()
+    pl.semaphore_wait(barrier, outer * inner - 1)
+
+    for unit in range(per):
+        for which in range(3):
+            for step in steps:
+                in_copy(unit, which, step, 1).start()
+
+    def compute(unit, block):
+        o_buf[unit, rows_of(block)] = attend_block(
+            q_buf[unit, rows_of(block)], k_buf[unit], v_buf[unit]
+        )
+
+    for unit in range(per):
+        for which in range(3):
+            own_copy(unit, which).wait()
+        for which in range(2):
+            for step in steps:
+                in_copy(unit, which, step, -1).wait_recv()
+
+        def one_block(index, carry):
+            step = jnp.where(index < half, index, index + 1)
+            in_copy(unit, 2, step, -1).wait_recv()
+            block = partner(step, -1)
+            compute(unit, block)
+            for part in range(inner):
+                out_copy(unit, block, part).start()
+            return carry
+
+        lax.fori_loop(0, outer - 1, one_block, 0)
+        compute(unit, me_o)
+        for shift in range(1, inner):
+            out_copy(unit, me_o, (me_i + shift) % inner).start()
+        out_own(unit).start()
+
+    for unit in range(per):
+        for which in range(3):
+            for step in steps:
+                in_copy(unit, which, step, 1).wait_send()
+
+        def sent(index, carry):
+            other = (me_o * inner + me_i + index) % (outer * inner)
+            out_copy(unit, other // inner, other % inner).wait_send()
+            return carry
+
+        lax.fori_loop(1, outer * inner, sent, 0)
+
+        def received(index, carry):
+            other = (me_o * inner + me_i + index) % (outer * inner)
+            slot = slot_of(other // inner, other % inner, unit)
+            pltpu.make_async_remote_copy(
+                src_ref=o_buf.at[unit, pl.ds(0, out_rows)],
+                dst_ref=out_ref.at[slot],
+                send_sem=out_send.at[unit, 0],
+                recv_sem=out_recv.at[slot],
+                device_id=(other // inner, other % inner),
+                device_id_type=MESH,
+            ).wait_recv()
+            return carry
+
+        lax.fori_loop(1, outer * inner, received, 0)
+        out_own(unit).wait()
+
+
+def per_device(outer, inner, queries, keys, values):
+    tokens, networks, local_cols = queries.shape
+    local_heads = local_cols // HEAD_DIM
+    pairs = networks * local_heads
+    per = pairs // outer
+    seq = tokens * outer
+    out_rows = tokens // inner
+    slots = pairs * inner
+
+    def by_pair(array):
+        split = array.reshape(tokens, networks, local_heads, HEAD_DIM)
+        return split.transpose(1, 2, 0, 3).reshape(pairs, tokens, HEAD_DIM)
+
+    buffer = pltpu.VMEM((per, seq, HEAD_DIM), jnp.bfloat16)
+    gathered = pl.pallas_call(
+        partial(exchange_kernel, outer, inner, networks, local_heads, per),
+        out_shape=jax.ShapeDtypeStruct((slots, out_rows, HEAD_DIM), jnp.bfloat16),
+        in_specs=[pl.BlockSpec(memory_space=pl.ANY)] * 3,
+        out_specs=pl.BlockSpec(memory_space=pl.ANY),
+        scratch_shapes=[
+            buffer, buffer, buffer, buffer,
+            pltpu.SemaphoreType.DMA((per * 3,)),
+            pltpu.SemaphoreType.DMA((per * 3, outer)),
+            pltpu.SemaphoreType.DMA((per * 3, outer)),
+            pltpu.SemaphoreType.DMA((per, outer * inner)),
+            pltpu.SemaphoreType.DMA((slots,)),
+        ],
+        compiler_params=pltpu.CompilerParams(collective_id=0, has_side_effects=True),
+    )(by_pair(queries), by_pair(keys), by_pair(values))
+    joined = gathered.reshape(networks, local_heads * inner, out_rows, HEAD_DIM)
+    return joined.transpose(2, 0, 1, 3).reshape(out_rows, networks, local_cols * inner)
 
 
 def solution(mesh):
+    outer, inner = mesh.shape["outer"], mesh.shape["inner"]
+
+    def body(queries, keys, values):
+        pairs = queries.shape[1] * queries.shape[2] // HEAD_DIM
+        if outer % 2 == 0 and pairs % outer == 0:
+            return per_device(outer, inner, queries, keys, values)
+        return per_device_split(queries, keys, values)
+
     return jax.shard_map(
-        per_device,
+        body,
         mesh=mesh,
-        in_specs=(P("outer", None, "inner"), P("outer", None, "inner"), P("outer", None, "inner")),
+        in_specs=(P("outer", None, "inner"),) * 3,
         out_specs=P(("outer", "inner"), None, None),
         check_vma=False,
     )

time: 147 us -> 62.8 us (0.43)
  blocking collectives: 98.5 us -> 0 us
  Pallas kernels: 0 us -> 55.2 us
  waiting for transfers between devices: 14.1 us -> 0 us
  between operations: 13.5 us -> 0.04 us
  matrix products: 4.86 us -> 0 us
  starting transfers between devices: 3.54 us -> 0 us
  local copies, waits for them, and re-layouts: 10 us -> 7.2 us
  other arithmetic: 1.62 us -> 0 us
    all_to_all x6 -> x0, blocking collectives: 98.5 us -> none  [the longest x1 20.5 us: per_device(): lax.all_to_all(flatten(full_k), 'outer', split_axis=1, concat_axis=0, til...]
    pallas_call x0 -> x1, Pallas kernels: none -> 55.2 us  [per_device(): pl.pallas_call(partial(exchange_kernel, outer, inner, networks, local_hea...]
    all_to_all x1 -> x0, waiting for transfers between devices: 14 us -> none  [per_device(): lax.all_to_all(flatten(full_q), 'outer', split_axis=1, concat_axis=0, til...]
    dynamic_slice x12 -> x0, local copies, waits for them, and re-layouts: 6.72 us -> none  [attend_piece(): running, unused = lax.scan(one_block, running, (key_blocks, value_blocks))]
    dot_general x8 -> x0, matrix products: 4.86 us -> none  [the longest x4 2.87 us: attend_keys(): jnp.einsum('qhk,khd->qhd', weights.astype(jnp.bfloat16), value_heads, pre...]
    reshape x1 -> x7, local copies, waits for them, and re-layouts: 1.13 us -> 5.73 us  [the longest x6 4.81 us: by_pair(): split = array.reshape(tokens, networks, local_heads, HEAD_DIM)]
    all_to_all x1 -> x0, starting transfers between devices: 3.49 us -> none  [per_device(): lax.all_to_all(flatten(full_q), 'outer', split_axis=1, concat_axis=0, til...]
  transfers between devices with their start and end apart: 3 -> 0, of which waited for: 1 -> 0; matrix products, arithmetic and copies ran while one was open for 1% -> 0% of each run, Pallas kernels for 0% -> 0%
where the time goes in v1:
time: 62.8 us; the launch traced here: 62.5 us
  Pallas kernels  55.2 us (88%)
  local copies, waits for them, and re-layouts  7.2 us (11%)
    pallas_call x1, Pallas kernels, per_device(): pl.pallas_call(partial(exchange_kernel, outer, inner, networks, local_hea...  55.2 us
    reshape x6, local copies, waits for them, and re-layouts, by_pair(): split = array.reshape(tokens, networks, local_heads, HEAD_DIM)  4.81 us

profile of v1, /device:TPU:0, one launch (start us, length us, event | category | flops | bytes accessed | tf_op | source)
XLA Modules:
  0.0 62.5 jit_solution(9005997003506796866)
XLA Ops:
  0.0 1.4 %reshape.24 = bf16[128,2,8,128]{3,2,1,0:T(8,128)(2,1)S(1)} reshape(bf16[128,2,1024]{2,1,0:T(2,128)(2,1)} %param.3) | data formatting | bytes 1048576 | tf_op jit(solution)/shard_map/reshape | solution.py:259
  1.4 0.0 copy-start
  1.4 0.9 %copy.4 = bf16[128,2,8,128]{3,0,2,1:T(8,128)(2,1)} copy(bf16[128,2,8,128]{3,2,1,0:T(8,128)(2,1)S(1)} %reshape.24) | data formatting | bytes 1048576 | tf_op jit(solution)/shard_map/reshape | solution.py:259
  2.3 0.1 copy-done
  2.4 0.3 reshape.26
  2.8 0.0 copy-start.1
  2.8 0.9 %copy.5 = bf16[128,2,8,128]{3,0,2,1:T(8,128)(2,1)} copy(bf16[128,2,8,128]{3,2,1,0:T(8,128)(2,1)S(1)} %reshape.26) | data formatting | bytes 1048576 | tf_op jit(solution)/shard_map/reshape | solution.py:259
  3.7 0.1 copy-done.1
  3.8 0.3 reshape.28
  4.1 0.9 %copy.6 = bf16[128,2,8,128]{3,0,2,1:T(8,128)(2,1)} copy(bf16[128,2,8,128]{3,2,1,0:T(8,128)(2,1)S(1)} %reshape.28) | data formatting | bytes 1048576 | tf_op jit(solution)/shard_map/reshape | solution.py:259
  5.1 55.2 %shard_map.37 = bf16[64,32,128]{2,1,0:T(8,128)(2,1)} custom-call(bf16[16,128,128]{2,1,0:T(8,128)(2,1)} %bitcast.14, bf16[16,128,128]{2,1,0:T(8,128)(2,1)} %bitcast.15, bf16[16,128,128]{2,1,0:T(8,128)(2,1)} %bitcast.16), custom_call_target="tpu_custom_call" | custom-call | tf_op jit(solution)/shard_map/pallas_call | solution.py:263
  60.3 1.2 %copy.7 = bf16[32,2,32,128]{3,2,1,0:T(8,128)(2,1)S(1)} copy(bf16[32,2,32,128]{3,0,2,1:T(8,128)(2,1)} %bitcast.17) | data formatting | bytes 1048576 | tf_op jit(solution)/shard_map/transpose | solution.py:279
  61.6 0.9 %reshape.31 = bf16[32,2,4096]{2,1,0:T(2,128)(2,1)} reshape(bf16[32,2,32,128]{3,2,1,0:T(8,128)(2,1)S(1)} %copy.7) | data formatting | bytes 1048576 | tf_op jit(solution)/shard_map/reshape | solution.py:279
Async XLA Ops:
  1.4 1.0 %copy-start = (bf16[128,2,1024]{2,1,0:T(2,128)(2,1)S(1)}, bf16[128,2,1024]{2,1,0:T(2,128)(2,1)}, u32[]{:S(2)}) copy-start(bf16[128,2,1024]{2,1,0:T(2,128)(2,1)} %param.4) | copy-start | bytes 1572868
  2.8 1.0 %copy-start.1 = (bf16[128,2,1024]{2,1,0:T(2,128)(2,1)S(1)}, bf16[128,2,1024]{2,1,0:T(2,128)(2,1)}, u32[]{:S(2)}) copy-start(bf16[128,2,1024]{2,1,0:T(2,128)(2,1)} %param.5) | copy-start | bytes 1572868

commit v2 on v1

--- a/solution.py
+++ b/solution.py
@@ -107,18 +107,17 @@
 
 
 def exchange_kernel(
-    outer, inner, networks, local_heads, per,
+    outer, inner, heads,
     q_ref, k_ref, v_ref, out_ref,
-    q_buf, k_buf, v_buf, o_buf,
+    q_raw, k_raw, v_raw, k_buf, v_buf, o_raw,
     local_sem, in_send, in_recv, out_send, out_recv,
 ):
     me_o, me_i = lax.axis_index("outer"), lax.axis_index("inner")
-    tokens = q_ref.shape[1]
-    out_rows = out_ref.shape[1]
-    all_heads = local_heads * inner
+    tokens, networks, local_cols = q_ref.shape
+    out_rows = out_ref.shape[0]
     half = outer // 2
     my_half, my_rest = me_o // half, me_o % half
-    refs, bufs = (k_ref, v_ref, q_ref), (k_buf, v_buf, q_buf)
+    refs, raws = (k_ref, v_ref, q_ref), (k_raw, v_raw, q_raw)
 
     def partner(step, sign):
         side = jnp.where(step < half, 1 - my_half, my_half)
@@ -127,47 +126,52 @@
     def rows_of(block):
         return pl.ds(pl.multiple_of(block * tokens, tokens), tokens)
 
+    def cols_of(head):
+        return pl.ds(pl.multiple_of(head * HEAD_DIM, HEAD_DIM), HEAD_DIM)
+
     steps = [step for step in range(outer) if step != half]
 
-    def in_copy(unit, which, step, sign):
+    def in_copy(head, which, step, sign):
         other = partner(step, sign)
         target = other if sign == 1 else me_o
         source = me_o if sign == 1 else other
         return pltpu.make_async_remote_copy(
-            src_ref=refs[which].at[target * per + unit],
-            dst_ref=bufs[which].at[unit, rows_of(source)],
-            send_sem=in_send.at[unit * 3 + which, step],
-            recv_sem=in_recv.at[unit * 3 + which, step],
+            src_ref=refs[which].at[:, :, cols_of(target * heads + head)],
+            dst_ref=raws[which].at[head, rows_of(source)],
+            send_sem=in_send.at[head * 3 + which, step],
+            recv_sem=in_recv.at[head * 3 + which, step],
             device_id=(other, me_i),
             device_id_type=MESH,
         )
 
-    def own_copy(unit, which):
+    def own_copy(head, which):
         return pltpu.make_async_copy(
-            refs[which].at[me_o * per + unit],
-            bufs[which].at[unit, rows_of(me_o)],
-            local_sem.at[unit * 3 + which],
-        )
-
-    def slot_of(source_o, source_i, unit):
-        pair = source_o * per + unit
-        return (pair // local_heads) * all_heads + source_i * local_heads + pair % local_heads
-
-    def out_copy(unit, block, part):
+            refs[which].at[:, :, cols_of(me_o * heads + head)],
+            raws[which].at[head, rows_of(me_o)],
+            local_sem.at[head * 3 + which],
+        )
+
+    def out_cols(source_o, source_i, head):
+        return cols_of(source_i * (local_cols // HEAD_DIM) + source_o * heads + head)
+
+    def out_slice(block, part):
+        return pl.ds(block * tokens + part * out_rows, out_rows)
+
+    def out_copy(head, block, part):
         return pltpu.make_async_remote_copy(
-            src_ref=o_buf.at[unit, pl.ds(pl.multiple_of(block * tokens + part * out_rows, out_rows), out_rows)],
-            dst_ref=out_ref.at[slot_of(me_o, me_i, unit)],
-            send_sem=out_send.at[unit, block * inner + part],
-            recv_sem=out_recv.at[slot_of(me_o, me_i, unit)],
+            src_ref=o_raw.at[head, out_slice(block, part)],
+            dst_ref=out_ref.at[:, :, out_cols(me_o, me_i, head)],
+            send_sem=out_send.at[head, block * inner + part],
+            recv_sem=out_recv.at[head, me_o * inner + me_i],
             device_id=(block, part),
             device_id_type=MESH,
         )
 
-    def out_own(unit):
+    def out_own(head):
         return pltpu.make_async_copy(
-            o_buf.at[unit, pl.ds(pl.multiple_of(me_o * tokens + me_i * out_rows, out_rows), out_rows)],
-            out_ref.at[slot_of(me_o, me_i, unit)],
-            out_recv.at[slot_of(me_o, me_i, unit)],
+            o_raw.at[head, out_slice(me_o, me_i)],
+            out_ref.at[:, :, out_cols(me_o, me_i, head)],
+            out_recv.at[head, me_o * inner + me_i],
         )
 
     barrier = pltpu.get_barrier_semaphore()
@@ -180,111 +184,132 @@
         return carry
 
     lax.fori_loop(1, outer * inner, greet, 0)
-    for unit in range(per):
+    for head in range(heads):
         for which in range(3):
-            own_copy(unit, which).start()
+            own_copy(head, which).start()
     pl.semaphore_wait(barrier, outer * inner - 1)
 
-    for unit in range(per):
+    for head in range(heads):
         for which in range(3):
             for step in steps:
-                in_copy(unit, which, step, 1).start()
-
-    def compute(unit, block):
-        o_buf[unit, rows_of(block)] = attend_block(
-            q_buf[unit, rows_of(block)], k_buf[unit], v_buf[unit]
-        )
-
-    for unit in range(per):
+                in_copy(head, which, step, 1).start()
+
+    both = networks * tokens
+    split_row = lax.broadcasted_iota(jnp.int32, (both, both), 0)
+    split_col = lax.broadcasted_iota(jnp.int32, (both, both), 1)
+    split = (split_col == (split_row % tokens) * networks + split_row // tokens)
+    split = split.astype(jnp.float32).astype(jnp.bfloat16)
+    join = (split_row == (split_col % tokens) * networks + split_col // tokens)
+    join = join.astype(jnp.float32).astype(jnp.bfloat16)
+
+    def separate(raw, head, block):
+        mixed = raw[head, rows_of(block)].reshape(both, HEAD_DIM)
+        return jnp.dot(split, mixed, preferred_element_type=jnp.float32).astype(jnp.bfloat16)
+
+    def place(head, which, block):
+        apart = separate(raws[which], head, block)
+        kept = (k_buf, v_buf)[which]
+        for network in range(networks):
+            kept[network, rows_of(block)] = apart[network * tokens:(network + 1) * tokens]
+
+    def compute(head, block):
+        query = separate(q_raw, head, block)
+        parts = [
+            attend_block(query[n * tokens:(n + 1) * tokens], k_buf[n], v_buf[n])
+            for n in range(networks)
+        ]
+        mixed = jnp.dot(join, jnp.concatenate(parts, axis=0), preferred_element_type=jnp.float32)
+        o_raw[head, rows_of(block)] = mixed.astype(jnp.bfloat16).reshape(
+            tokens, networks, HEAD_DIM
+        )
+
+    for head in range(heads):
         for which in range(3):
-            own_copy(unit, which).wait()
+            own_copy(head, which).wait()
         for which in range(2):
-            for step in steps:
-                in_copy(unit, which, step, -1).wait_recv()
+            place(head, which, me_o)
+
+            def one_place(index, carry):
+                step = jnp.where(index < half, index, index + 1)
+                in_copy(head, which, step, -1).wait_recv()
+                place(head, which, partner(step, -1))
+                return carry
+
+            lax.fori_loop(0, outer - 1, one_place, 0)
 
         def one_block(index, carry):
             step = jnp.where(index < half, index, index + 1)
-            in_copy(unit, 2, step, -1).wait_recv()
+            in_copy(head, 2, step, -1).wait_recv()
             block = partner(step, -1)
-            compute(unit, block)
+            compute(head, block)
             for part in range(inner):
-                out_copy(unit, block, part).start()
+                out_copy(head, block, part).start()
             return carry
 
         lax.fori_loop(0, outer - 1, one_block, 0)
-        compute(unit, me_o)
+        compute(head, me_o)
         for shift in range(1, inner):
-            out_copy(unit, me_o, (me_i + shift) % inner).start()
-        out_own(unit).start()
-
-    for unit in range(per):
+            out_copy(head, me_o, (me_i + shift) % inner).start()
+        out_own(head).start()
+
+    for head in range(heads):
         for which in range(3):
             for step in steps:
-                in_copy(unit, which, step, 1).wait_send()
+                in_copy(head, which, step, 1).wait_send()
 
         def sent(index, carry):
             other = (me_o * inner + me_i + index) % (outer * inner)
-            out_copy(unit, other // inner, other % inner).wait_send()
+            out_copy(head, other // inner, other % inner).wait_send()
             return carry
 
         lax.fori_loop(1, outer * inner, sent, 0)
 
         def received(index, carry):
             other = (me_o * inner + me_i + index) % (outer * inner)
-            slot = slot_of(other // inner, other % inner, unit)
             pltpu.make_async_remote_copy(
-                src_ref=o_buf.at[unit, pl.ds(0, out_rows)],
-                dst_ref=out_ref.at[slot],
-                send_sem=out_send.at[unit, 0],
-                recv_sem=out_recv.at[slot],
+                src_ref=o_raw.at[head, pl.ds(0, out_rows)],
+                dst_ref=out_ref.at[:, :, out_cols(other // inner, other % inner, head)],
+                send_sem=out_send.at[head, 0],
+                recv_sem=out_recv.at[head, other],
                 device_id=(other // inner, other % inner),
                 device_id_type=MESH,
             ).wait_recv()
             return carry
 
         lax.fori_loop(1, outer * inner, received, 0)
-        out_own(unit).wait()
+        out_own(head).wait()
 
 
 def per_device(outer, inner, queries, keys, values):
     tokens, networks, local_cols = queries.shape
-    local_heads = local_cols // HEAD_DIM
-    pairs = networks * local_heads
-    per = pairs // outer
+    heads = local_cols // HEAD_DIM // outer
     seq = tokens * outer
     out_rows = tokens // inner
-    slots = pairs * inner
-
-    def by_pair(array):
-        split = array.reshape(tokens, networks, local_heads, HEAD_DIM)
-        return split.transpose(1, 2, 0, 3).reshape(pairs, tokens, HEAD_DIM)
-
-    buffer = pltpu.VMEM((per, seq, HEAD_DIM), jnp.bfloat16)
-    gathered = pl.pallas_call(
-        partial(exchange_kernel, outer, inner, networks, local_heads, per),
-        out_shape=jax.ShapeDtypeStruct((slots, out_rows, HEAD_DIM), jnp.bfloat16),
+    raw = pltpu.VMEM((heads, seq, networks, HEAD_DIM), jnp.bfloat16)
+    kept = pltpu.VMEM((networks, seq, HEAD_DIM), jnp.bfloat16)
+    return pl.pallas_call(
+        partial(exchange_kernel, outer, inner, heads),
+        out_shape=jax.ShapeDtypeStruct((out_rows, networks, local_cols * inner), jnp.bfloat16),
         in_specs=[pl.BlockSpec(memory_space=pl.ANY)] * 3,
         out_specs=pl.BlockSpec(memory_space=pl.ANY),
         scratch_shapes=[
-            buffer, buffer, buffer, buffer,
-            pltpu.SemaphoreType.DMA((per * 3,)),
-            pltpu.SemaphoreType.DMA((per * 3, outer)),
-            pltpu.SemaphoreType.DMA((per * 3, outer)),
-            pltpu.SemaphoreType.DMA((per, outer * inner)),
-            pltpu.SemaphoreType.DMA((slots,)),
+            raw, raw, raw, kept, kept, raw,
+            pltpu.SemaphoreType.DMA((heads * 3,)),
+            pltpu.SemaphoreType.DMA((heads * 3, outer)),
+            pltpu.SemaphoreType.DMA((heads * 3, outer)),
+            pltpu.SemaphoreType.DMA((heads, outer * inner)),
+            pltpu.SemaphoreType.DMA((heads, outer * inner)),
         ],
         compiler_params=pltpu.CompilerParams(collective_id=0, has_side_effects=True),
-    )(by_pair(queries), by_pair(keys), by_pair(values))
-    joined = gathered.reshape(networks, local_heads * inner, out_rows, HEAD_DIM)
-    return joined.transpose(2, 0, 1, 3).reshape(out_rows, networks, local_cols * inner)
+    )(queries, keys, values)
 
 
 def solution(mesh):
     outer, inner = mesh.shape["outer"], mesh.shape["inner"]
 
     def body(queries, keys, values):
-        pairs = queries.shape[1] * queries.shape[2] // HEAD_DIM
-        if outer % 2 == 0 and pairs % outer == 0:
+        heads = queries.shape[2] // HEAD_DIM
+        if outer % 2 == 0 and heads % outer == 0:
             return per_device(outer, inner, queries, keys, values)
         return per_device_split(queries, keys, values)
 

time: 62.8 us -> 59.8 us (0.952)
  local copies, waits for them, and re-layouts: 7.2 us -> 2.28 us
  Pallas kernels: 55.2 us -> 57.3 us
    reshape x7 -> x0, local copies, waits for them, and re-layouts: 5.73 us -> none  [the longest x6 4.81 us: by_pair(): split = array.reshape(tokens, networks, local_heads, HEAD_DIM)]
    pallas_call x1, Pallas kernels: 55.2 us -> 57.3 us  [per_device(): pl.pallas_call(partial(exchange_kernel, outer, inner, heads), out_shape=j...]
    unnamed x4 -> x1, local copies, waits for them, and re-layouts: 0.22 us -> 2.28 us
    transpose x1 -> x0, local copies, waits for them, and re-layouts: 1.25 us -> none  [per_device(): joined.transpose(2, 0, 1, 3).reshape(out_rows, networks, local_cols * inner)]
where the time goes in v2:
time: 59.8 us; the launch traced here: 59.6 us
  Pallas kernels  57.3 us (96%)
  local copies, waits for them, and re-layouts  2.28 us (4%)
    pallas_call x1, Pallas kernels, per_device(): pl.pallas_call(partial(exchange_kernel, outer, inner, heads), out_shape=j...  57.3 us
    unnamed x1, local copies, waits for them, and re-layouts  2.28 us

profile of v2, /device:TPU:0, one launch (start us, length us, event | category | flops | bytes accessed | tf_op | source)
XLA Modules:
  0.0 59.6 jit_solution(17424746038969449287)
XLA Ops:
  0.0 57.3 %shard_map.37 = bf16[32,2,4096]{2,1,0:T(2,128)(2,1)} custom-call(bf16[128,2,1024]{2,1,0:T(2,128)(2,1)} %q_ref.1, bf16[128,2,1024]{2,1,0:T(2,128)(2,1)} %k_ref.1, bf16[128,2,1024]{2,1,0:T(2,128)(2,1)} %v_ref.1), custom_call_target="tpu_custom_call" | custom-call | tf_op jit(solution)/shard_map/pallas_call | solution.py:290
  57.4 2.3 %copy.5 = bf16[32,2,4096]{2,1,0:T(2,128)(2,1)} copy(bf16[32,2,4096]{2,1,0:T(2,128)(2,1)} %shard_map.37) | data formatting | bytes 1048576

commit v3 on v2

--- a/solution.py
+++ b/solution.py
@@ -110,14 +110,14 @@
     outer, inner, heads,
     q_ref, k_ref, v_ref, out_ref,
     q_raw, k_raw, v_raw, k_buf, v_buf, o_raw,
-    local_sem, in_send, in_recv, out_send, out_recv,
+    q_src, k_src, v_src, src_sem, local_sem, in_send, in_recv, out_send, out_recv,
 ):
     me_o, me_i = lax.axis_index("outer"), lax.axis_index("inner")
     tokens, networks, local_cols = q_ref.shape
     out_rows = out_ref.shape[0]
     half = outer // 2
     my_half, my_rest = me_o // half, me_o % half
-    refs, raws = (k_ref, v_ref, q_ref), (k_raw, v_raw, q_raw)
+    refs, raws = (k_src, v_src, q_src), (k_raw, v_raw, q_raw)
 
     def partner(step, sign):
         side = jnp.where(step < half, 1 - my_half, my_half)
@@ -138,7 +138,7 @@
         return pltpu.make_async_remote_copy(
             src_ref=refs[which].at[:, :, cols_of(target * heads + head)],
             dst_ref=raws[which].at[head, rows_of(source)],
-            send_sem=in_send.at[head * 3 + which, step],
+            send_sem=in_send,
             recv_sem=in_recv.at[head * 3 + which, step],
             device_id=(other, me_i),
             device_id_type=MESH,
@@ -161,8 +161,8 @@
         return pltpu.make_async_remote_copy(
             src_ref=o_raw.at[head, out_slice(block, part)],
             dst_ref=out_ref.at[:, :, out_cols(me_o, me_i, head)],
-            send_sem=out_send.at[head, block * inner + part],
-            recv_sem=out_recv.at[head, me_o * inner + me_i],
+            send_sem=out_send,
+            recv_sem=out_recv,
             device_id=(block, part),
             device_id_type=MESH,
         )
@@ -171,28 +171,33 @@
         return pltpu.make_async_copy(
             o_raw.at[head, out_slice(me_o, me_i)],
             out_ref.at[:, :, out_cols(me_o, me_i, head)],
-            out_recv.at[head, me_o * inner + me_i],
+            out_recv,
         )
 
     barrier = pltpu.get_barrier_semaphore()
 
-    def greet(index, carry):
-        other = (me_o * inner + me_i + index) % (outer * inner)
-        pl.semaphore_signal(
-            barrier, inc=1, device_id=(other // inner, other % inner), device_id_type=MESH
-        )
-        return carry
-
-    lax.fori_loop(1, outer * inner, greet, 0)
-    for head in range(heads):
-        for which in range(3):
-            own_copy(head, which).start()
+    sources = [
+        pltpu.make_async_copy(ref, kept, src_sem.at[which])
+        for which, (ref, kept) in enumerate(zip((k_ref, v_ref, q_ref), refs))
+    ]
+    for copy in sources:
+        copy.start()
+    ends = [partner(step, 1) for step in steps]
+    for shift in range(inner):
+        part = (me_i + shift) % inner
+        for other in ends:
+            pl.semaphore_signal(barrier, inc=1, device_id=(other, part), device_id_type=MESH)
+        if shift:
+            pl.semaphore_signal(barrier, inc=1, device_id=(me_o, part), device_id_type=MESH)
+    for copy in sources:
+        copy.wait()
     pl.semaphore_wait(barrier, outer * inner - 1)
 
     for head in range(heads):
         for which in range(3):
             for step in steps:
                 in_copy(head, which, step, 1).start()
+            own_copy(head, which).start()
 
     both = networks * tokens
     split_row = lax.broadcasted_iota(jnp.int32, (both, both), 0)
@@ -237,6 +242,11 @@
 
             lax.fori_loop(0, outer - 1, one_place, 0)
 
+        compute(head, me_o)
+        for shift in range(1, inner):
+            out_copy(head, me_o, (me_i + shift) % inner).start()
+        out_own(head).start()
+
         def one_block(index, carry):
             step = jnp.where(index < half, index, index + 1)
             in_copy(head, 2, step, -1).wait_recv()
@@ -247,37 +257,15 @@
             return carry
 
         lax.fori_loop(0, outer - 1, one_block, 0)
-        compute(head, me_o)
-        for shift in range(1, inner):
-            out_copy(head, me_o, (me_i + shift) % inner).start()
-        out_own(head).start()
+
+    def wait_bytes(ref, sem):
+        pltpu.make_async_copy(ref, ref, sem).wait()
 
     for head in range(heads):
-        for which in range(3):
-            for step in steps:
-                in_copy(head, which, step, 1).wait_send()
-
-        def sent(index, carry):
-            other = (me_o * inner + me_i + index) % (outer * inner)
-            out_copy(head, other // inner, other % inner).wait_send()
-            return carry
-
-        lax.fori_loop(1, outer * inner, sent, 0)
-
-        def received(index, carry):
-            other = (me_o * inner + me_i + index) % (outer * inner)
-            pltpu.make_async_remote_copy(
-                src_ref=o_raw.at[head, pl.ds(0, out_rows)],
-                dst_ref=out_ref.at[:, :, out_cols(other // inner, other % inner, head)],
-                send_sem=out_send.at[head, 0],
-                recv_sem=out_recv.at[head, other],
-                device_id=(other // inner, other % inner),
-                device_id_type=MESH,
-            ).wait_recv()
-            return carry
-
-        lax.fori_loop(1, outer * inner, received, 0)
-        out_own(head).wait()
+        for raw in raws:
+            wait_bytes(raw.at[head, pl.ds(0, tokens * (outer - 1))], in_send)
+        wait_bytes(o_raw.at[head, pl.ds(0, tokens * outer - out_rows)], out_send)
+    wait_bytes(out_ref, out_recv)
 
 
 def per_device(outer, inner, queries, keys, values):
@@ -294,11 +282,13 @@
         out_specs=pl.BlockSpec(memory_space=pl.ANY),
         scratch_shapes=[
             raw, raw, raw, kept, kept, raw,
+            *[pltpu.VMEM(queries.shape, jnp.bfloat16)] * 3,
+            pltpu.SemaphoreType.DMA((3,)),
             pltpu.SemaphoreType.DMA((heads * 3,)),
+            pltpu.SemaphoreType.DMA,
             pltpu.SemaphoreType.DMA((heads * 3, outer)),
-            pltpu.SemaphoreType.DMA((heads * 3, outer)),
-            pltpu.SemaphoreType.DMA((heads, outer * inner)),
-            pltpu.SemaphoreType.DMA((heads, outer * inner)),
+            pltpu.SemaphoreType.DMA,
+            pltpu.SemaphoreType.DMA,
         ],
         compiler_params=pltpu.CompilerParams(collective_id=0, has_side_effects=True),
     )(queries, keys, values)

time: 59.8 us -> 57 us (0.953)
  the two profiles are of different devices: /device:TPU:0 before, /device:TPU:29 now
where the time goes in v3:
time: 57 us; the launch traced here: 56.9 us
  Pallas kernels  54.6 us (96%)
  local copies, waits for them, and re-layouts  2.28 us (4%)
    pallas_call x1, Pallas kernels, per_device(): pl.pallas_call(partial(exchange_kernel, outer, inner, heads), out_shape=j...  54.6 us
    unnamed x1, local copies, waits for them, and re-layouts  2.28 us

profile of v3, /device:TPU:29, one launch (start us, length us, event | category | flops | bytes accessed | tf_op | source)
XLA Modules:
  0.0 56.9 jit_solution(13533017057062205146)
XLA Ops:
  0.0 54.6 %shard_map.37 = bf16[32,2,4096]{2,1,0:T(2,128)(2,1)} custom-call(bf16[128,2,1024]{2,1,0:T(2,128)(2,1)} %q_ref.1, bf16[128,2,1024]{2,1,0:T(2,128)(2,1)} %k_ref.1, bf16[128,2,1024]{2,1,0:T(2,128)(2,1)} %v_ref.1), custom_call_target="tpu_custom_call" | custom-call | tf_op jit(solution)/shard_map/pallas_call | solution.py:278
  54.6 2.3 %copy.5 = bf16[32,2,4096]{2,1,0:T(2,128)(2,1)} copy(bf16[32,2,4096]{2,1,0:T(2,128)(2,1)} %shard_map.37) | data formatting | bytes 1048576

commit v4 on v3

--- a/solution.py
+++ b/solution.py
@@ -290,7 +290,7 @@
             pltpu.SemaphoreType.DMA,
             pltpu.SemaphoreType.DMA,
         ],
-        compiler_params=pltpu.CompilerParams(collective_id=0, has_side_effects=True),
+        compiler_params=pltpu.CompilerParams(collective_id=0, has_side_effects=True, vmem_limit_bytes=54500 * 1024),
     )(queries, keys, values)
 
 

time: 57 us -> 55.5 us (0.974)
  the two profiles are of different devices: /device:TPU:29 before, /device:TPU:25 now
where the time goes in v4:
time: 55.5 us; the launch traced here: 55.3 us
  Pallas kernels  54.5 us (98%)
  local copies, waits for them, and re-layouts  0.8 us (1%)
    pallas_call x1, Pallas kernels, per_device(): pl.pallas_call(partial(exchange_kernel, outer, inner, heads), out_shape=j...  54.5 us

profile of v4, /device:TPU:25, one launch (start us, length us, event | category | flops | bytes accessed | tf_op | source)
XLA Modules:
  0.0 55.3 jit_solution(8641165062664368430)
XLA Ops:
  0.0 54.5 %shard_map.37 = bf16[32,2,4096]{2,1,0:T(2,128)(2,1)S(1)} custom-call(bf16[128,2,1024]{2,1,0:T(2,128)(2,1)} %q_ref.1, bf16[128,2,1024]{2,1,0:T(2,128)(2,1)} %k_ref.1, bf16[128,2,1024]{2,1,0:T(2,128)(2,1)} %v_ref.1), custom_call_target="tpu_custom_call" | custom-call | tf_op jit(solution)/shard_map/pallas_call | solution.py:278
  54.5 0.8 %copy.5 = bf16[32,2,4096]{2,1,0:T(2,128)(2,1)} copy(bf16[32,2,4096]{2,1,0:T(2,128)(2,1)S(1)} %shard_map.37) | data formatting | bytes 1048576
